TPU v7x, 8 devices: a whole 2x2x1 slice. The times are simulated.
8 devices in a mesh: data: 1 (over z), fsdp: 2 (over y), ep: 4 (over x, core).
Axes of the slice: x: 2, y: 2, z: 1, core: 2. Of those that a mesh axis runs over, the one named last changes fastest.
Arguments:
- tokens: bfloat16 [64, 512, 1024], P(('data', 'fsdp', 'ep'))
- w_qkv: bfloat16 [1024, 3, 16, 64], P('fsdp')
- w_out: bfloat16 [16, 64, 1024], P(None, None, 'fsdp')
- w_gate: bfloat16 [32, 1024, 512], P('ep', 'fsdp')
- w_up: bfloat16 [32, 1024, 512], P('ep', 'fsdp')
- w_down: bfloat16 [32, 512, 1024], P('ep', None, 'fsdp')
- expert_idx: int32 [64, 512, 8], P(('data', 'fsdp', 'ep'))
- expert_slot: int32 [64, 512, 8], P(('data', 'fsdp', 'ep'))
- gate_wts: bfloat16 [64, 512, 8], P(('data', 'fsdp', 'ep'))
- d_out: bfloat16 [64, 512, 1024], P(('data', 'fsdp', 'ep'))
Outputs:
- output 1: bfloat16 [64, 512, 1024], P(('data', 'fsdp', 'ep'))
- output 2: bfloat16 [64, 512, 1024], P(('data', 'fsdp', 'ep'))
- output 3: float32 [32, 1024, 512], P(('data', 'ep'), 'fsdp')
- output 4: float32 [32, 1024, 512], P(('data', 'ep'), 'fsdp')
- output 5: float32 [32, 512, 1024], P(('data', 'ep'), None, 'fsdp')
All inputs are finite; a program needn't handle non-finite values.
Results may differ from a plain program's by a relative error of at most 0.02.
Values are sent between devices in bfloat16 or wider.
A program may use at most 1 GiB of HBM per device.

v0:
```python
import jax
import jax.numpy as jnp
from jax import lax
from jax.sharding import PartitionSpec as P, NamedSharding


def rms_norm(values):
    wide_vals = values.astype(jnp.float32)
    inv_rms = lax.rsqrt(jnp.mean(wide_vals * wide_vals, axis=-1, keepdims=True) + 1e-6)
    return (wide_vals * inv_rms).astype(jnp.bfloat16)


def attention_block(tok_seq, w_qkv, w_out):
    seq_len = tok_seq.shape[1]
    head_dim = w_qkv.shape[3]
    normed = rms_norm(tok_seq)
    qkv_all = jnp.einsum('bsd,dthe->tbshe', normed, w_qkv, preferred_element_type=jnp.float32).astype(jnp.bfloat16)
    scores = jnp.einsum('bqhe,bkhe->bhqk', qkv_all[0], qkv_all[1], preferred_element_type=jnp.float32) * (head_dim ** -0.5)
    causal = lax.broadcasted_iota(jnp.int32, (seq_len, seq_len), 0) >= lax.broadcasted_iota(jnp.int32, (seq_len, seq_len), 1)
    attn_probs = jax.nn.softmax(jnp.where(causal, scores, -1e30), axis=-1).astype(jnp.bfloat16)
    context = jnp.einsum('bhqk,bkhe->bqhe', attn_probs, qkv_all[2], preferred_element_type=jnp.float32).astype(jnp.bfloat16)
    attn_proj = jnp.einsum('crif,ife->cre', context, w_out, preferred_element_type=jnp.float32)
    return (tok_seq.astype(jnp.float32) + attn_proj).astype(jnp.bfloat16)


def capacity_of(tok_count, top_k, num_experts):
    return max(8, (5 * tok_count * top_k // (4 * num_experts) + 7) // 8 * 8)


def route_maps(idx_one, slot_one, num_experts, capacity):
    n_assign = idx_one.size
    flat_slot = slot_one.reshape(n_assign)
    row_pos = jnp.where(flat_slot >= 0, idx_one.reshape(n_assign) * capacity + flat_slot, num_experts * capacity)
    src_assign = jnp.full((num_experts * capacity,), n_assign, jnp.int32).at[row_pos].set(jnp.arange(n_assign, dtype=jnp.int32), mode='drop')
    return row_pos, src_assign


def gather_experts(w_gate, w_up, w_down):
    gate_full = lax.all_gather(w_gate, 'fsdp', axis=1, tiled=True)
    up_full = lax.all_gather(w_up, 'fsdp', axis=1, tiled=True)
    down_full = lax.all_gather(w_down, 'fsdp', axis=2, tiled=True)
    return gate_full, up_full, down_full


def solution(mesh):
    ep_size = mesh.shape['ep']
    tok_spec = P(('data', 'fsdp', 'ep'))
    in_specs = (tok_spec, P('fsdp'), P(None, None, 'fsdp'), P('ep', 'fsdp'), P('ep', 'fsdp'), P('ep', None, 'fsdp'), tok_spec, tok_spec, tok_spec, tok_spec)
    out_specs = (tok_spec, tok_spec, P(('data', 'ep'), 'fsdp'), P(('data', 'ep'), 'fsdp'), P(('data', 'ep'), None, 'fsdp'))

    def device_fn(tokens, w_qkv, w_out, w_gate, w_up, w_down, expert_idx, expert_slot, gate_wts, d_out):
        n_seq, seq_len, d_model = tokens.shape
        tok_count = n_seq * seq_len
        top_k = expert_idx.shape[2]
        local_experts = w_gate.shape[0]
        num_experts = local_experts * ep_size
        capacity = capacity_of(tok_count, top_k, num_experts)
        buf_shape = (ep_size, local_experts, capacity, d_model)
        qkv_full = lax.all_gather(w_qkv, 'fsdp', axis=0, tiled=True)
        out_full = lax.all_gather(w_out, 'fsdp', axis=2, tiled=True)
        h_seq, attn_pullback = jax.vjp(lambda tok_in: attention_block(tok_in, qkv_full, out_full), tokens)
        h_tok = h_seq.reshape(tok_count, d_model)
        u_tok, norm_pullback = jax.vjp(rms_norm, h_tok)
        row_pos, src_assign = route_maps(expert_idx, expert_slot, num_experts, capacity)
        src_tok = src_assign // top_k
        gate_full, up_full, down_full = gather_experts(w_gate, w_up, w_down)
        disp_buf = jnp.take(u_tok, src_tok, axis=0, mode='fill', fill_value=0).reshape(buf_shape)
        recv_u = lax.all_to_all(disp_buf, 'ep', 0, 0, tiled=True)
        act_a = jnp.einsum('sncd,ndf->sncf', recv_u, gate_full, preferred_element_type=jnp.float32)
        act_b = jnp.einsum('sncd,ndf->sncf', recv_u, up_full, preferred_element_type=jnp.float32)
        gated_act = (jax.nn.silu(act_a) * act_b).astype(jnp.bfloat16)
        y_exp = jnp.einsum('sncf,nfd->sncd', gated_act, down_full, preferred_element_type=jnp.float32).astype(jnp.bfloat16)
        y_back = lax.all_to_all(y_exp, 'ep', 0, 0, tiled=True).reshape(num_experts * capacity, d_model)
        y_rows = jnp.take(y_back, row_pos, axis=0, mode='fill', fill_value=0).reshape(tok_count, top_k, d_model)
        gate_tok = gate_wts.reshape(tok_count, top_k)
        mixed_sum = jnp.einsum('tk,tkd->td', gate_tok, y_rows, preferred_element_type=jnp.float32)
        layer_out = (h_tok.astype(jnp.float32) + mixed_sum).astype(jnp.bfloat16).reshape(n_seq, seq_len, d_model)
        dout_tok = d_out.reshape(tok_count, d_model)
        gate_sel = jnp.take(gate_tok.reshape(tok_count * top_k), src_assign, axis=0, mode='fill', fill_value=0)
        dy_buf = (jnp.take(dout_tok, src_tok, axis=0, mode='fill', fill_value=0) * gate_sel[:, None]).reshape(buf_shape)
        dy_recv = lax.all_to_all(dy_buf, 'ep', 0, 0, tiled=True)
        gate_again, up_again, down_again = gather_experts(w_gate, w_up, w_down)
        d_gated = jnp.einsum('sncd,nfd->sncf', dy_recv, down_again, preferred_element_type=jnp.float32)
        sig_a = jax.nn.sigmoid(act_a)
        d_up_act = (d_gated * act_a * sig_a).astype(jnp.bfloat16)
        d_gate_act = (d_gated * act_b * sig_a * (1.0 + act_a * (1.0 - sig_a))).astype(jnp.bfloat16)
        dw_down = jnp.einsum('sncf,sncd->nfd', gated_act, dy_recv, preferred_element_type=jnp.float32)
        dw_gate = jnp.einsum('sncd,sncf->ndf', recv_u, d_gate_act, preferred_element_type=jnp.float32)
        dw_up = jnp.einsum('sncd,sncf->ndf', recv_u, d_up_act, preferred_element_type=jnp.float32)
        d_recv = (jnp.einsum('sncf,ndf->sncd', d_gate_act, gate_again, preferred_element_type=jnp.float32) + jnp.einsum('sncf,ndf->sncd', d_up_act, up_again, preferred_element_type=jnp.float32)).astype(jnp.bfloat16)
        d_disp = lax.all_to_all(d_recv, 'ep', 0, 0, tiled=True).reshape(num_experts * capacity, d_model)
        du_rows = jnp.take(d_disp, row_pos, axis=0, mode='fill', fill_value=0).reshape(tok_count, top_k, d_model)
        d_u = jnp.sum(du_rows, axis=1, dtype=jnp.float32).astype(jnp.bfloat16)
        d_h_norm = norm_pullback(d_u)[0]
        d_h = (dout_tok.astype(jnp.float32) + d_h_norm.astype(jnp.float32)).astype(jnp.bfloat16).reshape(n_seq, seq_len, d_model)
        d_tokens = attn_pullback(d_h)[0]
        dw_gate_part = lax.psum_scatter(dw_gate, 'fsdp', scatter_dimension=1, tiled=True)
        dw_up_part = lax.psum_scatter(dw_up, 'fsdp', scatter_dimension=1, tiled=True)
        dw_down_part = lax.psum_scatter(dw_down, 'fsdp', scatter_dimension=2, tiled=True)
        return layer_out, d_tokens, dw_gate_part, dw_up_part, dw_down_part

    return jax.shard_map(device_fn, mesh=mesh, in_specs=in_specs, out_specs=out_specs, check_vma=False)
```

profile of v0, /device:TPU:7, one launch (start us, length us, event | category | flops | bytes accessed | tf_op | source)
XLA Modules:
  0.0 6264.4 jit_solution(12842020057706108126)
XLA Ops:
  7.2 0.7 all-gather.6.cloned.1.call-update
  7.9 0.7 all-gather.8.cloned.1.call-update
  8.6 0.8 iota_compare_fusion
  9.4 1.0 add_select_fusion.2
  11.0 1.1 select_n.65
  12.3 120.7 %scatter_custom_fusion = s32[40960]{0:T(1024)S(1)} fusion(s32[32768]{0:T(1024)S(1)} %bitcast.251, s32[32768]{0:T(1024)S(1)} %iota.19, s32[]{:T(128)} %constant.50.clone.1), kind=kCustom, calls=%fused_computation.151 | custom fusion | bytes 163844 | tf_op jit(solution)/shard_map/scatter | solution.py:34
  133.0 0.8 compare_and_fusion
  133.8 0.8 fusion.102
  134.6 5.1 fusion.50
  140.9 1.3 copy.42
  142.3 1.1 reshape_reshape.3
  143.3 251.6 %gather_fusion = bf16[40960]{0:T(1024)(128)(2,1)S(1)} fusion(bf16[32768]{0:T(1024)(128)(2,1)S(1)} %reshape_reshape.3, s32[40960]{0:T(1024)} %get-tuple-element.10), kind=kCustom, calls=%fused_computation.4 | custom fusion | bytes 327680 | tf_op jit(solution)/shard_map/jit(_take)/gather | solution.py:79
  394.9 0.7 and_select_fusion
  395.6 203.2 %gather_fusion.3 = bf16[40960,1024]{1,0:T(8,128)(2,1)} fusion(bf16[4096,1024]{1,0:T(8,128)(2,1)} %bitcast.245, s32[40960]{0:T(1024)S(1)} %get-tuple-element.11), kind=kCustom, calls=%fused_computation.2.clone | custom fusion | bytes 167936000 | tf_op jit(solution)/shard_map/jit(_take)/gather | solution.py:80
  598.8 34.4 convert_bitcast_fusion
  633.2 57.3 fusion.115
  690.5 63.8 %divide_convert_fusion = bf16[8,16,512,512]{2,3,1,0:T(8,128)(2,1)} fusion(f32[8,16,512,512]{2,3,1,0:T(8,128)} %get-tuple-element.17, f32[8,16,512]{2,1,0:T(8,128)S(1)} %get-tuple-element.16), kind=kLoop, calls=%fused_computation.16 | loop fusion | flops 67108864 | bytes 201588736 | tf_op jit(solution)/shard_map/jvp()/convert_element_type | solution.py:20
  754.3 29.1 fusion.85.clone.4
  783.4 17.4 fusion.55
  800.8 0.6 fusion.107
  801.5 8.2 fusion.56
  809.7 203.1 %gather_fusion.1 = bf16[40960,1024]{1,0:T(8,128)(2,1)} fusion(bf16[4096,1024]{1,0:T(8,128)(2,1)} %fusion.56, s32[40960]{0:T(1024)S(1)} %copy-done.7), kind=kCustom, calls=%fused_computation.clone | custom fusion | bytes 167936000 | tf_op jit(solution)/shard_map/jit(_take)/gather | solution.py:67
  1012.8 108.9 %select_multiply_fusion = (bf16[40960,1024]{1,0:T(8,128)(2,1)}, bf16[40960,1024]{1,0:T(8,128)(2,1)}) fusion(bf16[40960,1024]{1,0:T(8,128)(2,1)} %gather_fusion.3, pred[40960]{0:T(1024)(128)(4,1)S(1)} %copy-done.17, bf16[40960]{0:T(1024)(128)(2,1)S(1)} %copy-done.13, bf16[40960,1024]{1,0:T(8,128)(2,1)} %gather_fusion.1), kind=kLoop, calls=%fused_computation.39 | loop fusion | flops 125829120 | bytes 335667200 | tf_op jit(solution)/shard_map/mul | solution.py:80
  1121.7 940.3 %all_to_all.20 = bf16[4,8,1280,1024]{3,2,1,0:T(8,128)(2,1)} all-to-all(bf16[4,8,1280,1024]{3,2,1,0:T(8,128)(2,1)} %bitcast.13), channel_id=1, replica_groups=mesh['data'=1,'fsdp'=2,'ep'=4] {'ep'}, dimensions={0} | all-to-all | bytes 167772160 | tf_op jit(solution)/shard_map/all_to_all | solution.py:68
  2062.0 18.9 all-to-all-start.2
  2080.9 0.7 all-gather.12.cloned.1.call-update
  2082.8 102.2 %all-gather.12.cloned.1.call-done = bf16[8,1024,512]{2,1,0:T(8,128)(2,1)} async-done(((bf16[8,512,512]{2,1,0:T(8,128)(2,1)}), bf16[8,1024,512]{2,1,0:T(8,128)(2,1)}) %all-gather.12.cloned.1.call-update) | async-done | bytes 8388624 | tf_op jit(solution)/shard_map/all_gather | solution.py:40
  2185.0 70.9 %fusion.24 = f32[8,4,1280,512]{3,2,1,0:T(8,128)} fusion(bf16[4,8,1280,1024]{3,2,1,0:T(8,128)(2,1)} %all_to_all.20, bf16[8,1024,512]{2,1,0:T(8,128)(2,1)} %all-gather.12.cloned.1.call-done), kind=kOutput, calls=%fused_computation.45 | convolution fusion | flops 42949672960 | bytes 176160768 | tf_op jit(solution)/shard_map/sncd,ndf->sncf/dot_general | solution.py:70
  2255.9 32.8 all-gather.10.cloned.1.call-done
  2288.7 70.2 %fusion.26 = f32[8,4,1280,512]{3,2,1,0:T(8,128)} fusion(bf16[4,8,1280,1024]{3,2,1,0:T(8,128)(2,1)} %all_to_all.20, bf16[8,1024,512]{2,1,0:T(8,128)(2,1)} %all-gather.10.cloned.1.call-done), kind=kOutput, calls=%fused_computation.47 | convolution fusion | flops 42949672960 | bytes 176160768 | tf_op jit(solution)/shard_map/sncd,ndf->sncf/dot_general | solution.py:69
  2358.9 33.4 all-gather.14.cloned.1.call-done
  2392.3 588.7 %all-to-all-done.2 = bf16[4,8,1280,1024]{3,2,1,0:T(8,128)(2,1)} async-done(((bf16[4,8,1280,1024]{3,2,1,0:T(8,128)(2,1)}), bf16[4,8,1280,1024]{3,2,1,0:T(8,128)(2,1)}, u32[]{:S(2)}, u32[]{:S(2)}) %all-to-all-start.2) | async-done | bytes 83886112 | tf_op jit(solution)/shard_map/all_to_all | solution.py:81
  2981.0 136.3 %fusion.14 = (bf16[4,8,1280,512]{3,2,0,1:T(8,128)(2,1)}, bf16[4,8,1280,512]{3,2,0,1:T(8,128)(2,1)}, bf16[4,8,1280,512]{3,2,0,1:T(8,128)(2,1)}) fusion(f32[8,4,1280,512]{3,2,1,0:T(8,128)} %fusion.26, f32[8,4,1280,512]{3,2,1,0:T(8,128)} %fusion.24, bf16[8,512,1024]{2,1,0:T(8,128)(2,1)} %all-gather.14.cloned.1.call-done, ...), kind=kOutput, calls=%fused_computation.29 | convolution fusion | flops 43285217280 | bytes 385875968 | tf_op jit(solution)/shard_map/sncd,nfd->sncf/dot_general | solution.py:83
  3117.3 77.0 %fusion.80 = f32[8,4,1280,1024]{3,2,1,0:T(8,128)} fusion(bf16[4,8,1280,512]{3,2,0,1:T(8,128)(2,1)} %get-tuple-element.8, bf16[8,1024,512]{2,1,0:T(8,128)(2,1)} %all-gather.10.cloned.1.call-done), kind=kOutput, calls=%fused_computation.113 | convolution fusion | flops 42949672960 | bytes 218103808 | tf_op jit(solution)/shard_map/sncf,ndf->sncd/dot_general | solution.py:90
  3194.4 97.6 %fusion.9 = bf16[4,8,1280,1024]{3,2,0,1:T(8,128)(2,1)} fusion(f32[8,4,1280,1024]{3,2,1,0:T(8,128)} %fusion.80, bf16[4,8,1280,512]{3,2,0,1:T(8,128)(2,1)} %get-tuple-element.7, bf16[8,1024,512]{2,1,0:T(8,128)(2,1)} %all-gather.12.cloned.1.call-done), kind=kOutput, calls=%fused_computation.22 | convolution fusion | flops 43033559040 | bytes 301989888 | tf_op jit(solution)/shard_map/sncf,ndf->sncd/dot_general | solution.py:90
  3291.9 55.4 copy.44
  3347.4 18.9 all-to-all-start.3
  3366.3 57.0 fusion.59
  3423.5 57.6 fusion.64
  3481.1 1.0 select_n.68
  3482.2 3.8 copy.58
  3486.0 0.6 compare_and_fusion.1
  3486.7 0.7 fusion.103
  3487.3 0.7 multiply_divide_fusion
  3488.1 56.2 fusion.8
  3544.3 55.4 copy.41
  3599.7 666.7 %all-to-all-done.3 = bf16[4,8,1280,1024]{3,2,1,0:T(8,128)(2,1)} async-done(((bf16[4,8,1280,1024]{3,2,1,0:T(8,128)(2,1)}), bf16[4,8,1280,1024]{3,2,1,0:T(8,128)(2,1)}, u32[]{:S(2)}, u32[]{:S(2)}) %all-to-all-start.3) | async-done | bytes 83886112 | tf_op jit(solution)/shard_map/all_to_all | solution.py:91
  4266.4 18.9 all-to-all-start.1
  4285.3 57.1 fusion.67
  4342.5 746.5 %gather_fusion.4 = bf16[32768,1024]{1,0:T(8,128)(2,1)} fusion(bf16[40960,1024]{1,0:T(8,128)(2,1)} %bitcast.36, s32[32768]{0:T(1024)S(1)} %copy-done.8), kind=kCustom, calls=%fused_computation.3.clone | custom fusion | bytes 134348800 | tf_op jit(solution)/shard_map/jit(_take)/gather | solution.py:92
  5089.0 52.3 bitcast_reduce_fusion
  5141.2 8.2 fusion.47
  5149.4 10.5 add_convert_fusion.1
  5159.9 3.3 copy-done.1
  5163.2 9.5 fusion.92
  5172.8 74.5 %fusion.6 = (f32[8,16,512]{2,1,0:T(8,128)S(1)}, bf16[8,16,512,512]{2,3,1,0:T(8,128)(2,1)}) fusion(f32[8,16,512,512]{2,3,1,0:T(8,128)} %get-tuple-element.17, f32[8,16,512]{2,1,0:T(8,128)S(1)} %copy-done.5, bf16[3,8,512,16,64]{2,4,3,0,1:T(8,128)(2,1)} %convert_bitcast_fusion, bf16[8,512,16,64]{1,3,2,0:T(8,128)(2,1)S(1)} %fusion.92), kind=kOutput, calls=%fused_computation.15 | convolution fusion | flops 4462673920 | bytes 218628096 | tf_op jit(solution)/shard_map/transpose(jvp(bhqk,bkhe->bqhe))/dot_general | solution.py:21
  5247.3 68.0 %convert_bitcast_fusion.2 = bf16[1,8,512,16,64]{2,4,3,1,0:T(8,128)(2,1)} fusion(bf16[3,8,512,16,64]{2,4,3,0,1:T(8,128)(2,1)} %convert_bitcast_fusion, f32[8,16,512,512]{2,3,1,0:T(8,128)} %get-tuple-element.17, bf16[8,16,512,512]{2,3,1,0:T(8,128)(2,1)} %get-tuple-element.21, f32[8,16,512]{2,1,0:T(8,128)S(1)} %neg.12, f32[8,16,512]{2,1,0:T(8,128)S(1)} %copy-done.12, ...), kind=kOutput, calls=%fused_computation.120 | convolution fusion | flops 4500488192 | bytes 218890240 | tf_op jit(solution)/shard_map/transpose(jvp(bqhe,bkhe->bhqk))/dot_general | solution.py:18
  5315.3 67.7 %convert_bitcast_fusion.1 = bf16[1,8,512,16,64]{2,4,3,1,0:T(8,128)(2,1)} fusion(bf16[3,8,512,16,64]{2,4,3,0,1:T(8,128)(2,1)} %convert_bitcast_fusion, f32[8,16,512,512]{2,3,1,0:T(8,128)} %get-tuple-element.17, bf16[8,16,512,512]{2,3,1,0:T(8,128)(2,1)} %get-tuple-element.21, f32[8,16,512]{2,1,0:T(8,128)S(1)} %neg.12, f32[8,16,512]{2,1,0:T(8,128)S(1)} %copy-done.12, ...), kind=kOutput, calls=%fused_computation.119 | convolution fusion | flops 4500488192 | bytes 218890240 | tf_op jit(solution)/shard_map/transpose(jvp(bqhe,bkhe->bhqk))/dot_general | solution.py:18
  5383.0 741.5 %gather_fusion.2 = bf16[32768,1024]{1,0:T(8,128)(2,1)} fusion(bf16[40960,1024]{1,0:T(8,128)(2,1)} %bitcast.23, s32[32768]{0:T(1024)S(1)} %copy-done.9), kind=kCustom, calls=%fused_computation.1.clone | custom fusion | bytes 134348800 | tf_op jit(solution)/shard_map/jit(_take)/gather | solution.py:74
  6124.5 34.1 convert_bitcast_fusion.3
  6158.5 34.8 fusion.53
  6193.4 39.2 fusion.28
  6232.6 13.4 fusion.54
  6246.1 11.2 fusion.72
  (87 shorter events, 3.5 us)
Async XLA Ops:
  7.2 591.6 %all-gather.6.cloned.1.call-start = ((), (), s32[]{:S(2)}) async-start(), calls=%async_computation.7 | async-start | bytes 9437184 | tf_op jit(solution)/shard_map/all_gather | solution.py:59
  7.9 775.5 %all-gather.8.cloned.1.call-start = ((), (), s32[]{:S(2)}) async-start(), calls=%async_computation.8 | async-start | bytes 3145728 | tf_op jit(solution)/shard_map/all_gather | solution.py:60
  11.0 129.9 %copy-start.2 = (s32[8,512,8]{2,1,0:T(8,128)}, s32[8,512,8]{2,1,0:T(8,128)S(1)}, u32[]{:S(2)}) copy-start(s32[8,512,8]{2,1,0:T(8,128)S(1)} %copy.37) | copy-start | bytes 393220
  134.6 261.0 %copy-start.6 = (s32[40960]{0:T(1024)}, s32[40960]{0:T(1024)S(1)}, u32[]{:S(2)}) copy-start(s32[40960]{0:T(1024)S(1)} %get-tuple-element.11) | copy-start | bytes 491524
  139.7 0.6 copy-start.18
  395.6 203.2 %copy-start.23 = (f32[8,512]{1,0:T(8,128)S(1)}, f32[8,512]{1,0:T(8,128)}, u32[]{:S(2)}) copy-start(f32[8,512]{1,0:T(8,128)} %fusion.106) | copy-start | bytes 49156
  598.8 34.4 copy-start.15
  690.5 63.8 %copy-start.10 = (f32[8,16,512]{2,1,0:T(8,128)}, f32[8,16,512]{2,1,0:T(8,128)S(1)}, u32[]{:S(2)}) copy-start(f32[8,16,512]{2,1,0:T(8,128)S(1)} %get-tuple-element.16) | copy-start | bytes 786436
  783.4 26.2 copy-start.7
  800.8 0.6 copy-start.25
  809.7 203.1 %copy-start.13 = (bf16[40960]{0:T(1024)(128)(2,1)S(1)}, bf16[40960]{0:T(1024)(128)(2,1)}, u32[]{:S(2)}) copy-start(bf16[40960]{0:T(1024)(128)(2,1)} %and_select_fusion) | copy-start | bytes 245764
  809.7 203.1 %copy-start.17 = (pred[40960]{0:T(1024)(128)(4,1)S(1)}, pred[40960]{0:T(1024)(128)(4,1)}, u32[]{:S(2)}) copy-start(pred[40960]{0:T(1024)(128)(4,1)} %compare_and_fusion) | copy-start | bytes 122884
  2062.0 919.0 %all-to-all-start.2 = ((bf16[4,8,1280,1024]{3,2,1,0:T(8,128)(2,1)}), bf16[4,8,1280,1024]{3,2,1,0:T(8,128)(2,1)}, u32[]{:S(2)}, u32[]{:S(2)}) async-start(bf16[4,8,1280,1024]{3,2,1,0:T(8,128)(2,1)} %bitcast.30), calls=%async_computation.2 | async-start | bytes 167772160 | tf_op jit(solution)/shard_map/all_to_all | solution.py:81
  2080.9 104.1 %all-gather.12.cloned.1.call-start = ((), (), s32[]{:S(2)}) async-start(), calls=%async_computation.10 | async-start | bytes 12582912 | tf_op jit(solution)/shard_map/all_gather | solution.py:40
  2081.6 207.0 %all-gather.10.cloned.1.call-start = ((), (), s32[]{:S(2)}) async-start(), calls=%async_computation.9 | async-start | bytes 12582912 | tf_op jit(solution)/shard_map/all_gather | solution.py:39
  2082.2 310.1 %all-gather.14.cloned.1.call-start = ((), (), s32[]{:S(2)}) async-start(), calls=%async_computation.11 | async-start | bytes 12582912 | tf_op jit(solution)/shard_map/all_gather | solution.py:41
  3347.4 919.0 %all-to-all-start.3 = ((bf16[4,8,1280,1024]{3,2,1,0:T(8,128)(2,1)}), bf16[4,8,1280,1024]{3,2,1,0:T(8,128)(2,1)}, u32[]{:S(2)}, u32[]{:S(2)}) async-start(bf16[4,8,1280,1024]{3,2,1,0:T(8,128)(2,1)} %copy.44), calls=%async_computation.3 | async-start | bytes 167772160 | tf_op jit(solution)/shard_map/all_to_all | solution.py:91
  3366.3 2891.0 %reduce-scatter.8.cloned.1.call-start = ((), (), s32[]{:S(2)}) async-start(), calls=%async_computation.14 | async-start | bytes 25165824 | tf_op jit(solution)/shard_map/reduce_scatter | solution.py:99
  3423.4 57.7 copy-start.3
  3423.4 58.8 copy-start.14
  3423.4 63.9 %copy-start.11 = (f32[8,16,512]{2,1,0:T(8,128)S(1)}, f32[8,16,512]{2,1,0:T(8,128)}, u32[]{:S(2)}) copy-start(f32[8,16,512]{2,1,0:T(8,128)} %copy-done.10) | copy-start | bytes 786436
  3423.4 2833.9 %reduce-scatter.4.cloned.1.call-start = ((), (), s32[]{:S(2)}) async-start(), calls=%async_computation.12 | async-start | bytes 25165824 | tf_op jit(solution)/shard_map/reduce_scatter | solution.py:97
  4266.4 1116.6 %all-to-all-start.1 = ((bf16[4,8,1280,1024]{3,2,1,0:T(8,128)(2,1)}), bf16[4,8,1280,1024]{3,2,1,0:T(8,128)(2,1)}, u32[]{:S(2)}, u32[]{:S(2)}) async-start(bf16[4,8,1280,1024]{3,2,1,0:T(8,128)(2,1)} %copy.41), calls=%async_computation.1 | async-start | bytes 167772160 | tf_op jit(solution)/shard_map/all_to_all | solution.py:73
  4285.3 57.1 copy-start.8
  4285.3 1972.0 %reduce-scatter.6.cloned.1.call-start = ((), (), s32[]{:S(2)}) async-start(), calls=%async_computation.13 | async-start | bytes 25165824 | tf_op jit(solution)/shard_map/reduce_scatter | solution.py:98
  4342.5 746.5 %copy-start.20 = (pred[32768]{0:T(1024)(128)(4,1)S(1)}, pred[32768]{0:T(1024)(128)(4,1)}, u32[]{:S(2)}) copy-start(pred[32768]{0:T(1024)(128)(4,1)} %compare_and_fusion.1) | copy-start | bytes 98308
  5089.0 60.4 copy-start.26
  5089.0 60.5 copy-start.22
  5141.2 22.0 copy-start.27
  5159.9 3.3 copy-start.1
  5163.2 9.5 copy-start.5
  5172.8 74.5 %copy-start = (bf16[8,512,16,64]{1,3,2,0:T(8,128)(2,1)}, bf16[8,512,16,64]{1,3,2,0:T(8,128)(2,1)S(1)}, u32[]{:S(2)}) copy-start(bf16[8,512,16,64]{1,3,2,0:T(8,128)(2,1)S(1)} %fusion.92) | copy-start | bytes 25165828
  5172.8 74.5 %copy-start.12 = (f32[8,16,512]{2,1,0:T(8,128)S(1)}, f32[8,16,512]{2,1,0:T(8,128)}, u32[]{:S(2)}) copy-start(f32[8,16,512]{2,1,0:T(8,128)} %copy-done.10) | copy-start | bytes 786436
  5172.8 74.5 %copy-start.16 = (pred[512,512]{0,1:T(8,128)(4,1)S(1)}, pred[512,512]{0,1:T(8,128)(4,1)}, u32[]{:S(2)}) copy-start(pred[512,512]{0,1:T(8,128)(4,1)} %iota_compare_fusion) | copy-start | bytes 786436
  5315.3 67.7 %copy-start.9 = (s32[32768]{0:T(1024)S(1)}, s32[32768]{0:T(1024)}, u32[]{:S(2)}) copy-start(s32[32768]{0:T(1024)} %fusion.103) | copy-start | bytes 393220
  6158.5 34.8 copy-start.19
  6158.5 34.9 copy-start.21
  6158.5 74.1 %slice-start = ((s8[8388608]{0:T(1024)(128)(4,1)}), s8[4194304]{0:T(1024)(128)(4,1)S(1)}, s32[]{:S(2)}) async-start(s8[8388608]{0:T(1024)(128)(4,1)} %bitcast.246), calls=%async_computation.15 | async-start | bytes 8388608
  6193.4 39.2 slice-start.1
  6232.6 13.4 copy-start.4
  6232.6 13.4 copy-start.24
Sparse Core Ops, SparseCore 0:
  9.5 77.9 all-gather.5
  89.0 30.1 all-gather.7
  2083.2 101.7 all-gather.11
  2186.4 102.2 all-gather.9
  2290.0 102.2 all-gather.13
  3423.5 185.7 reduce-scatter.7
  3612.2 186.3 reduce-scatter.3
  4342.6 185.7 reduce-scatter.5
where the time goes:
time: 6350 us; the launch traced here: 6260 us
  local copies, waits for them, and re-layouts  2390 us (38%)
  waiting for transfers between devices  1430 us (23%)
  matrix products  1150 us (18%)
  blocking collectives  940 us (15%)
  other arithmetic  289 us (5%)
    all_to_all x1, blocking collectives, device_fn(): recv_u = lax.all_to_all(disp_buf, 'ep', 0, 0, tiled=True)  940 us
    gather x1, local copies, waits for them, and re-layouts, device_fn(): jnp.take(d_disp, row_pos, axis=0, mode='fill', fill_value=0)  746 us
    gather x1, local copies, waits for them, and re-layouts, device_fn(): jnp.take(y_back, row_pos, axis=0, mode='fill', fill_value=0)  742 us
    all_to_all x1, waiting for transfers between devices, device_fn(): lax.all_to_all(d_recv, 'ep', 0, 0, tiled=True)  667 us
    all_to_all x1, waiting for transfers between devices, device_fn(): dy_recv = lax.all_to_all(dy_buf, 'ep', 0, 0, tiled=True)  589 us
    gather x1, local copies, waits for them, and re-layouts, device_fn(): jnp.take(gate_tok.reshape(tok_count * top_k), src_assign, axis=0, mode='f...  252 us
    gather x1, local copies, waits for them, and re-layouts, device_fn(): jnp.take(dout_tok, src_tok, axis=0, mode='fill', fill_value=0)  203 us
    gather x1, local copies, waits for them, and re-layouts, device_fn(): jnp.take(u_tok, src_tok, axis=0, mode='fill', fill_value=0)  203 us
  transfers between devices with their start and end apart: 11, of which 5 were waited for; matrix products, arithmetic and copies ran while one was open for 50% of the time, Pallas kernels for 0%

commit v1 on v0

v1 whole, which is shorter than its diff:
```python
import functools

import jax
import jax.numpy as jnp
from jax import lax
from jax.experimental import pallas as pl
from jax.experimental.pallas import tpu as pltpu
from jax.sharding import PartitionSpec as P

F32 = jnp.float32
BF16 = jnp.bfloat16
BLOCK = 256
TILE = 256
ALIGN = 16
EPS = 1e-6


def rms_norm(values):
    wide_vals = values.astype(F32)
    inv_rms = lax.rsqrt(jnp.mean(wide_vals * wide_vals, axis=-1, keepdims=True) + EPS)
    return (wide_vals * inv_rms).astype(BF16)


def attention_block(tok_seq, w_qkv, w_out):
    seq_len = tok_seq.shape[1]
    head_dim = w_qkv.shape[3]
    normed = rms_norm(tok_seq)
    qkv_all = jnp.einsum('bsd,dthe->tbshe', normed, w_qkv, preferred_element_type=F32).astype(BF16)
    scores = jnp.einsum('bqhe,bkhe->bhqk', qkv_all[0], qkv_all[1], preferred_element_type=F32) * (head_dim ** -0.5)
    causal = lax.broadcasted_iota(jnp.int32, (seq_len, seq_len), 0) >= lax.broadcasted_iota(jnp.int32, (seq_len, seq_len), 1)
    attn_probs = jax.nn.softmax(jnp.where(causal, scores, -1e30), axis=-1).astype(BF16)
    context = jnp.einsum('bhqk,bkhe->bqhe', attn_probs, qkv_all[2], preferred_element_type=F32).astype(BF16)
    attn_proj = jnp.einsum('crif,ife->cre', context, w_out, preferred_element_type=F32)
    return (tok_seq.astype(F32) + attn_proj).astype(BF16)


def capacity_of(tok_count, top_k, num_experts):
    return max(8, (5 * tok_count * top_k // (4 * num_experts) + 7) // 8 * 8)


def route(expert_idx, expert_slot, num_experts):
    n_seq, seq_len, top_k = expert_idx.shape
    per_seq = seq_len // BLOCK

    def blocks(values):
        values = values.transpose(0, 2, 1).reshape(n_seq, top_k, per_seq, BLOCK)
        return values.transpose(0, 2, 1, 3).reshape(n_seq * per_seq, top_k, BLOCK)

    idx_b, slot_b = blocks(expert_idx), blocks(expert_slot)
    kept = slot_b >= 0
    ids = jnp.arange(num_experts, dtype=jnp.int32)[None, :, None]
    member = jnp.zeros((idx_b.shape[0], num_experts, BLOCK), BF16)
    for j in range(top_k):
        member = member + ((idx_b[:, j:j + 1] == ids) & kept[:, j:j + 1]).astype(BF16)
    upper = (jnp.arange(BLOCK)[:, None] <= jnp.arange(BLOCK)[None, :]).astype(BF16)
    count = jnp.einsum('bet,ts->bes', member, upper, preferred_element_type=F32).astype(jnp.int32)
    seg_rows = (count[:, :, -1] + (ALIGN - 1)) // ALIGN * ALIGN
    seg_start = jnp.cumsum(seg_rows, axis=1) - seg_rows
    seg_off = jnp.cumsum(seg_rows, axis=0) - seg_rows
    place = seg_start[:, :, None] + count - 1
    dest = []
    for j in range(top_k):
        hit = (idx_b[:, j:j + 1] == ids)
        row = jnp.sum(jnp.where(hit, place, 0), axis=1)
        dest.append(jnp.where(kept[:, j], row, -1))
    dest = jnp.stack(dest, axis=1)
    return dest, seg_start, seg_rows, seg_off


def one_hot(dest_ref, gate_ref, first_row):
    rows = lax.broadcasted_iota(jnp.int32, (TILE, BLOCK), 0) + first_row
    dest = dest_ref[0]
    gate = gate_ref[0]
    picked = jnp.zeros((TILE, BLOCK), F32)
    for j in range(dest.shape[0]):
        picked = jnp.where(rows == dest[j:j + 1], gate[j:j + 1], picked)
    return picked


def dispatch_kernel(start_ref, rows_ref, off_ref, h_ref, dout_ref, dest_ref, gate_ref, r_hbm, d_hbm, u_s, rbuf, dbuf, sem):
    b = pl.program_id(0)
    n_blocks = pl.num_programs(0)
    n_exp = rows_ref.shape[1]
    slot = lax.rem(b, 2)

    def total(blk):
        return start_ref[blk, n_exp - 1] + rows_ref[blk, n_exp - 1]

    def drain(blk, which):
        n = pl.multiple_of(total(blk), ALIGN)

        @pl.when(n > 0)
        def _():
            pltpu.make_async_copy(rbuf.at[which, pl.ds(0, n), :], rbuf.at[which, pl.ds(0, n), :], sem.at[0, which]).wait()
            pltpu.make_async_copy(dbuf.at[which, pl.ds(0, n), :], dbuf.at[which, pl.ds(0, n), :], sem.at[1, which]).wait()

    @pl.when(b >= 2)
    def _():
        drain(b - 2, slot)

    hf = h_ref[...].astype(F32)
    u_s[...] = (hf * lax.rsqrt(jnp.mean(hf * hf, axis=-1, keepdims=True) + EPS)).astype(BF16)

    def tile(i, carry):
        first = pl.multiple_of(i * TILE, TILE)
        picked = one_hot(dest_ref, gate_ref, first)
        ones = jnp.where(picked > 0, 1.0, 0.0).astype(BF16)
        rbuf[slot, pl.ds(first, TILE), :] = jnp.dot(ones, u_s[...], preferred_element_type=F32).astype(BF16)
        dbuf[slot, pl.ds(first, TILE), :] = jnp.dot(picked.astype(BF16), dout_ref[...], preferred_element_type=F32).astype(BF16)
        return carry

    lax.fori_loop(0, (total(b) + (TILE - 1)) // TILE, tile, 0)

    def send(e, carry):
        n = pl.multiple_of(rows_ref[b, e], ALIGN)
        src = pl.multiple_of(start_ref[b, e], ALIGN)
        dst = pl.multiple_of(off_ref[b, e], ALIGN)

        @pl.when(n > 0)
        def _():
            pltpu.make_async_copy(rbuf.at[slot, pl.ds(src, n), :], r_hbm.at[e, pl.ds(dst, n), :], sem.at[0, slot]).start()
            pltpu.make_async_copy(dbuf.at[slot, pl.ds(src, n), :], d_hbm.at[e, pl.ds(dst, n), :], sem.at[1, slot]).start()
        return carry

    lax.fori_loop(0, n_exp, send, 0)

    @pl.when(b == n_blocks - 1)
    def _():
        @pl.when(n_blocks > 1)
        def _():
            drain(b - 1, 1 - slot)
        drain(b, slot)


def dispatch(h_tok, dout_tok, dest, gate, segs, num_experts, max_rows):
    tok_count, d_model = h_tok.shape
    n_blocks, top_k, _ = dest.shape
    buf_rows = -(-(BLOCK * top_k + num_experts * (ALIGN - 1)) // TILE) * TILE
    tok_spec = pl.BlockSpec((BLOCK, d_model), lambda b, *_: (b, 0))
    map_spec = pl.BlockSpec((1, top_k, BLOCK), lambda b, *_: (b, 0, 0))
    rows_shape = jax.ShapeDtypeStruct((num_experts, max_rows, d_model), BF16)
    return pl.pallas_call(
        dispatch_kernel,
        grid_spec=pltpu.PrefetchScalarGridSpec(
            num_scalar_prefetch=3,
            grid=(n_blocks,),
            in_specs=[tok_spec, tok_spec, map_spec, map_spec],
            out_specs=[pl.BlockSpec(memory_space=pl.ANY), pl.BlockSpec(memory_space=pl.ANY)],
            scratch_shapes=[
                pltpu.VMEM((BLOCK, d_model), BF16),
                pltpu.VMEM((2, buf_rows, d_model), BF16),
                pltpu.VMEM((2, buf_rows, d_model), BF16),
                pltpu.SemaphoreType.DMA((2, 2)),
            ],
        ),
        out_shape=[rows_shape, rows_shape],
        compiler_params=pltpu.CompilerParams(dimension_semantics=('arbitrary',), vmem_limit_bytes=60 * 2 ** 20),
        cost_estimate=pl.CostEstimate(flops=80 * 10 ** 9, bytes_accessed=180 * 10 ** 6, transcendentals=0),
        name='dispatch',
    )(*segs, h_tok, dout_tok, dest, gate)


def nt_dot(lhs, rhs):
    return lax.dot_general(lhs, rhs, (((1,), (1,)), ((), ())), preferred_element_type=F32)


def tn_dot(lhs, rhs):
    return lax.dot_general(lhs, rhs, (((0,), (0,)), ((), ())), preferred_element_type=F32)


def expert_kernel(count_ref, r_ref, d_ref, w_ref, y_ref, dr_ref, dw_ref, *, expert_of):
    n_rows = count_ref[expert_of(pl.program_id(0))]
    dw_ref[...] = jnp.zeros(dw_ref.shape, F32)
    half = w_ref.shape[-1]

    def tile(i, carry):
        first = pl.multiple_of(i * TILE, TILE)
        valid = lax.broadcasted_iota(jnp.int32, (TILE, 1), 0) + first < n_rows
        r = jnp.where(valid, r_ref[0, pl.ds(first, TILE), :], 0)
        dy = jnp.where(valid, d_ref[0, pl.ds(first, TILE), :], 0)
        w1 = jnp.concatenate([w_ref[0, 0, 0, 0], w_ref[1, 0, 0, 0]], axis=0)
        w3 = jnp.concatenate([w_ref[0, 0, 1, 0], w_ref[1, 0, 1, 0]], axis=0)
        w2 = jnp.concatenate([w_ref[0, 0, 2, 0], w_ref[1, 0, 2, 0]], axis=1)
        act_a = jnp.dot(r, w1, preferred_element_type=F32)
        act_b = jnp.dot(r, w3, preferred_element_type=F32)
        d_g = nt_dot(dy, w2)
        sig = 1.0 / (1.0 + jnp.exp(-act_a))
        silu = act_a * sig
        g = (silu * act_b).astype(BF16)
        d_up = (d_g * silu).astype(BF16)
        d_gate = (d_g * act_b * sig * (1.0 + act_a * (1.0 - sig))).astype(BF16)
        y_ref[0, pl.ds(first, TILE), :] = jnp.dot(g, w2, preferred_element_type=F32).astype(BF16)
        dr_ref[0, pl.ds(first, TILE), :] = (nt_dot(d_gate, w1) + nt_dot(d_up, w3)).astype(BF16)
        r_lo, r_hi = r[:, :half], r[:, half:]
        dw_ref[0, 0, 0, 0] += tn_dot(r_lo, d_gate)
        dw_ref[1, 0, 0, 0] += tn_dot(r_hi, d_gate)
        dw_ref[0, 0, 1, 0] += tn_dot(r_lo, d_up)
        dw_ref[1, 0, 1, 0] += tn_dot(r_hi, d_up)
        dw_ref[0, 0, 2, 0] += tn_dot(g, dy[:, :half])
        dw_ref[1, 0, 2, 0] += tn_dot(g, dy[:, half:])
        return carry

    lax.fori_loop(0, (n_rows + (TILE - 1)) // TILE, tile, 0)


def experts(rows, d_rows, weights, counts, chunk, per_chunk, local_experts):
    _, max_rows, d_model = rows.shape
    n_fsdp, n_ep, three, _, half, _ = weights.shape

    def expert_of(g):
        return g // per_chunk * local_experts + chunk * per_chunk + lax.rem(g, per_chunk)

    row_spec = pl.BlockSpec((1, max_rows, d_model), lambda g, *_: (expert_of(g), 0, 0))
    w_spec = pl.BlockSpec((n_fsdp, 1, three, 1, half, half), lambda g, *_: (0, g // per_chunk, 0, lax.rem(g, per_chunk), 0, 0))
    return pl.pallas_call(
        functools.partial(expert_kernel, expert_of=expert_of),
        grid_spec=pltpu.PrefetchScalarGridSpec(
            num_scalar_prefetch=1,
            grid=(n_ep * per_chunk,),
            in_specs=[row_spec, row_spec, w_spec],
            out_specs=[row_spec, row_spec, w_spec],
        ),
        out_shape=[
            jax.ShapeDtypeStruct(rows.shape, BF16),
            jax.ShapeDtypeStruct(rows.shape, BF16),
            jax.ShapeDtypeStruct(weights.shape, F32),
        ],
        input_output_aliases={1: 0, 2: 1},
        compiler_params=pltpu.CompilerParams(dimension_semantics=('arbitrary',), vmem_limit_bytes=62 * 2 ** 20),
        cost_estimate=pl.CostEstimate(flops=110 * 10 ** 9, bytes_accessed=200 * 10 ** 6, transcendentals=0),
        name='experts',
    )(counts, rows, d_rows, weights)


def combine_kernel(start_ref, rows_ref, off_ref, y_hbm, dr_hbm, h_ref, dout_ref, dest_ref, gate_ref, out_ref, dh_ref, ybuf, dbuf, acc_y, acc_d, sem):
    b = pl.program_id(0)
    n_blocks = pl.num_programs(0)
    n_exp = rows_ref.shape[1]
    slot = lax.rem(b, 2)

    def total(blk):
        return start_ref[blk, n_exp - 1] + rows_ref[blk, n_exp - 1]

    def fetch(blk, which):
        def one(e, carry):
            n = pl.multiple_of(rows_ref[blk, e], ALIGN)
            dst = pl.multiple_of(start_ref[blk, e], ALIGN)
            src = pl.multiple_of(off_ref[blk, e], ALIGN)

            @pl.when(n > 0)
            def _():
                pltpu.make_async_copy(y_hbm.at[e, pl.ds(src, n), :], ybuf.at[which, pl.ds(dst, n), :], sem.at[0, which]).start()
                pltpu.make_async_copy(dr_hbm.at[e, pl.ds(src, n), :], dbuf.at[which, pl.ds(dst, n), :], sem.at[1, which]).start()
            return carry

        lax.fori_loop(0, n_exp, one, 0)

    @pl.when(b == 0)
    def _():
        ybuf[...] = jnp.zeros(ybuf.shape, BF16)
        dbuf[...] = jnp.zeros(dbuf.shape, BF16)
        fetch(0, 0)

    @pl.when(b + 1 < n_blocks)
    def _():
        fetch(b + 1, 1 - slot)

    n = pl.multiple_of(total(b), ALIGN)

    @pl.when(n > 0)
    def _():
        pltpu.make_async_copy(ybuf.at[slot, pl.ds(0, n), :], ybuf.at[slot, pl.ds(0, n), :], sem.at[0, slot]).wait()
        pltpu.make_async_copy(dbuf.at[slot, pl.ds(0, n), :], dbuf.at[slot, pl.ds(0, n), :], sem.at[1, slot]).wait()

    acc_y[...] = jnp.zeros(acc_y.shape, F32)
    acc_d[...] = jnp.zeros(acc_d.shape, F32)

    def tile(i, carry):
        first = pl.multiple_of(i * TILE, TILE)
        picked = one_hot(dest_ref, gate_ref, first)
        ones = jnp.where(picked > 0, 1.0, 0.0).astype(BF16)
        acc_y[...] += tn_dot(picked.astype(BF16), ybuf[slot, pl.ds(first, TILE), :])
        acc_d[...] += tn_dot(ones, dbuf[slot, pl.ds(first, TILE), :])
        return carry

    lax.fori_loop(0, (n + (TILE - 1)) // TILE, tile, 0)

    hf = h_ref[...].astype(F32)
    out_ref[...] = (hf + acc_y[...]).astype(BF16)
    d_u = acc_d[...].astype(BF16).astype(F32)
    inv = lax.rsqrt(jnp.mean(hf * hf, axis=-1, keepdims=True) + EPS)
    proj = jnp.mean(d_u * hf, axis=-1, keepdims=True)
    d_norm = (d_u * inv - hf * (inv * inv * inv * proj)).astype(BF16).astype(F32)
    dh_ref[...] = (dout_ref[...].astype(F32) + d_norm).astype(BF16)


def combine(y_rows, dr_rows, h_tok, dout_tok, dest, gate, segs):
    tok_count, d_model = h_tok.shape
    n_blocks, top_k, _ = dest.shape
    num_experts = y_rows.shape[0]
    buf_rows = -(-(BLOCK * top_k + num_experts * (ALIGN - 1)) // TILE) * TILE
    tok_spec = pl.BlockSpec((BLOCK, d_model), lambda b, *_: (b, 0))
    map_spec = pl.BlockSpec((1, top_k, BLOCK), lambda b, *_: (b, 0, 0))
    hbm = pl.BlockSpec(memory_space=pl.ANY)
    return pl.pallas_call(
        combine_kernel,
        grid_spec=pltpu.PrefetchScalarGridSpec(
            num_scalar_prefetch=3,
            grid=(n_blocks,),
            in_specs=[hbm, hbm, tok_spec, tok_spec, map_spec, map_spec],
            out_specs=[tok_spec, tok_spec],
            scratch_shapes=[
                pltpu.VMEM((2, buf_rows, d_model), BF16),
                pltpu.VMEM((2, buf_rows, d_model), BF16),
                pltpu.VMEM((BLOCK, d_model), F32),
                pltpu.VMEM((BLOCK, d_model), F32),
                pltpu.SemaphoreType.DMA((2, 2)),
            ],
        ),
        out_shape=[jax.ShapeDtypeStruct((tok_count, d_model), BF16)] * 2,
        compiler_params=pltpu.CompilerParams(dimension_semantics=('arbitrary',), vmem_limit_bytes=60 * 2 ** 20),
        cost_estimate=pl.CostEstimate(flops=90 * 10 ** 9, bytes_accessed=180 * 10 ** 6, transcendentals=0),
        name='combine',
    )(*segs, y_rows, dr_rows, h_tok, dout_tok, dest, gate)


N_CHUNKS = 4


def solution(mesh):
    ep_size, fsdp_size = mesh.shape['ep'], mesh.shape['fsdp']
    tok_spec = P(('data', 'fsdp', 'ep'))
    in_specs = (tok_spec, P('fsdp'), P(None, None, 'fsdp'), P('ep', 'fsdp'), P('ep', 'fsdp'), P('ep', None, 'fsdp'), tok_spec, tok_spec, tok_spec, tok_spec)
    out_specs = (tok_spec, tok_spec, P(('data', 'ep'), 'fsdp'), P(('data', 'ep'), 'fsdp'), P(('data', 'ep'), None, 'fsdp'))

    def device_fn(tokens, w_qkv, w_out, w_gate, w_up, w_down, expert_idx, expert_slot, gate_wts, d_out):
        n_seq, seq_len, d_model = tokens.shape
        tok_count = n_seq * seq_len
        top_k = expert_idx.shape[2]
        local_experts, half, _ = w_gate.shape
        num_experts = local_experts * ep_size
        n_blocks = tok_count // BLOCK
        capacity = capacity_of(tok_count, top_k, num_experts)
        max_rows = -(-(capacity + n_blocks * (ALIGN - 1)) // TILE) * TILE
        per_chunk = local_experts // N_CHUNKS

        qkv_full = lax.all_gather(w_qkv, 'fsdp', axis=0, tiled=True)
        out_full = lax.all_gather(w_out, 'fsdp', axis=2, tiled=True)
        weights = []
        for c in range(N_CHUNKS):
            part = slice(c * per_chunk, (c + 1) * per_chunk)
            mine = jnp.stack([w_gate[part], w_up[part], w_down[part]], axis=0)
            full = lax.all_gather(mine, ('fsdp', 'ep'), axis=0, tiled=False)
            weights.append(full.reshape(fsdp_size, ep_size, *mine.shape))

        dest, *segs = route(expert_idx, expert_slot, num_experts)
        counts = jnp.sum(segs[1], axis=0)
        gate = gate_wts.transpose(0, 2, 1).reshape(n_seq, top_k, seq_len // BLOCK, BLOCK)
        gate = gate.transpose(0, 2, 1, 3).reshape(n_blocks, top_k, BLOCK).astype(F32)

        h_seq, attn_pullback = jax.vjp(lambda tok_in: attention_block(tok_in, qkv_full, out_full), tokens)
        h_tok = h_seq.reshape(tok_count, d_model)
        dout_tok = d_out.reshape(tok_count, d_model)
        rows, d_rows = dispatch(h_tok, dout_tok, dest, gate, segs, num_experts, max_rows)
        parts = []
        for c in range(N_CHUNKS):
            rows, d_rows, d_w = experts(rows, d_rows, weights[c], counts, c, per_chunk, local_experts)
            d_w = d_w.reshape(fsdp_size * ep_size, 3, per_chunk, half, half)
            parts.append(lax.psum_scatter(d_w, ('fsdp', 'ep'), scatter_dimension=0, tiled=False))
        layer_out, d_h = combine(rows, d_rows, h_tok, dout_tok, dest, gate, segs)
        d_tokens = attn_pullback(d_h.reshape(n_seq, seq_len, d_model))[0]
        d_ws = [jnp.concatenate([part[k] for part in parts], axis=0) for k in range(3)]
        return layer_out.reshape(n_seq, seq_len, d_model), d_tokens, *d_ws

    return jax.shard_map(device_fn, mesh=mesh, in_specs=in_specs, out_specs=out_specs, check_vma=False)
```

time: 6350 us -> 1750 us (0.28); the launches traced: 6260 us -> 1740 us
  local copies, waits for them, and re-layouts: 2390 us -> 44 us
  waiting for transfers between devices: 1430 us -> 452 us
  blocking collectives: 940 us -> 0 us
  matrix products: 1150 us -> 427 us
  Pallas kernels: 0 us -> 645 us
  other arithmetic: 289 us -> 160 us
    gather x5 -> x0, local copies, waits for them, and re-layouts: 2150 us -> none  [the longest x1 746 us: device_fn(): jnp.take(d_disp, row_pos, axis=0, mode='fill', fill_value=0)]
    all_to_all x3 -> x0, waiting for transfers between devices: 1260 us -> none  [the longest x1 667 us: device_fn(): lax.all_to_all(d_recv, 'ep', 0, 0, tiled=True)]
    all_to_all x1 -> x0, blocking collectives: 940 us -> none  [device_fn(): recv_u = lax.all_to_all(disp_buf, 'ep', 0, 0, tiled=True)]
    dot_general x14 -> x5, matrix products: 815 us -> 99.1 us  [the longest x2 69.7 us: attention_block(): jnp.einsum('bsd,dthe->tbshe', normed, w_qkv, preferred_element_type=F32)]
    pallas_call x0 -> x6, Pallas kernels: none -> 645 us  [the longest x4 459 us: experts(): pl.pallas_call(functools.partial(expert_kernel, expert_of=expert_of), gri...]
    reduce_scatter x3 -> x4, waiting for transfers between devices: 0.02 us -> 451 us  [device_fn(): lax.psum_scatter(d_w, ('fsdp', 'ep'), scatter_dimension=0, tiled=False)]
    all_gather x3 -> x4, waiting for transfers between devices: 168 us -> 0.06 us  [device_fn(): full = lax.all_gather(mine, ('fsdp', 'ep'), axis=0, tiled=False)]
    scatter x1 -> x0, local copies, waits for them, and re-layouts: 121 us -> none  [route_maps(): jnp.full((num_experts * capacity,), n_assign, jnp.int32).at[row_pos]]
  transfers between devices with their start and end apart: 11 -> 10, of which waited for: 5 -> 2; matrix products, arithmetic and copies ran while one was open for 50% -> 35% of each run, Pallas kernels for 0% -> 37%
where the time goes in v1:
time: 1750 us; the launch traced here: 1740 us
  Pallas kernels  645 us (37%)
  waiting for transfers between devices  452 us (26%)
  matrix products  427 us (24%)
  other arithmetic  160 us (9%)
  local copies, waits for them, and re-layouts  44 us (3%)
    pallas_call x4, Pallas kernels, experts(): pl.pallas_call(functools.partial(expert_kernel, expert_of=expert_of), gri...  459 us
    reduce_scatter x4, waiting for transfers between devices, device_fn(): lax.psum_scatter(d_w, ('fsdp', 'ep'), scatter_dimension=0, tiled=False)  451 us
    dot_general x2, matrix products, attention_block(): jnp.einsum('bqhe,bkhe->bhqk', qkv_all[0], qkv_all[1], preferred_element_t...  136 us
    dot_general x3, matrix products, attention_block(): jnp.einsum('bhqk,bkhe->bqhe', attn_probs, qkv_all[2], preferred_element_t...  134 us
    pallas_call x1, Pallas kernels, combine(): pl.pallas_call(combine_kernel, grid_spec=pltpu.PrefetchScalarGridSpec(num...  101 us
    pallas_call x1, Pallas kernels, dispatch(): pl.pallas_call(dispatch_kernel, grid_spec=pltpu.PrefetchScalarGridSpec(nu...  84.9 us
    dot_general x2, matrix products, attention_block(): jnp.einsum('bsd,dthe->tbshe', normed, w_qkv, preferred_element_type=F32)  69.7 us
    convert_element_type x1, other arithmetic, attention_block(): jax.nn.softmax(jnp.where(causal, scores, -1e+30), axis=-1).astype(BF16)  63.8 us
  transfers between devices with their start and end apart: 10, of which 2 were waited for; matrix products, arithmetic and copies ran while one was open for 35% of the time, Pallas kernels for 37%

profile of v1, /device:TPU:7, one launch (start us, length us, event | category | flops | bytes accessed | tf_op | source)
XLA Modules:
  0.0 1744.3 jit_solution(15384040652084929654)
XLA Ops:
  7.2 0.7 all-gather.11.cloned.1.call-update
  7.9 0.7 all-gather.13.cloned.1.call-update
  8.7 4.1 slice_bitcast_fusion.32
  12.9 1.7 copy-done.11
  14.6 1.9 slice_bitcast_fusion.30
  16.4 2.0 pad_maximum_fusion.3
  18.5 3.9 pad_maximum_fusion.4
  22.5 3.6 pad_maximum_fusion.5
  26.1 3.3 pad_maximum_fusion.6
  29.4 0.5 reduce-scatter.5.cloned.1.call-start
  29.9 0.8 iota_compare_fusion.8
  31.9 0.1 copy.106
  33.0 9.3 fusion.61
  42.3 0.4 fusion.68
  42.8 1.3 copy.84
  44.1 0.1 convert_element_type.110
  44.3 1.3 copy-done.12
  45.6 0.6 fusion.87
  46.2 0.2 reduce_window_sum.24
  46.4 5.1 fusion.19
  51.6 0.5 copy-done.22
  52.1 0.7 convert.1.gate_ref
  52.8 0.7 fusion.78
  53.5 40.8 %select_reduce_fusion = (s32[16,256]{0,1:T(8,128)}, s32[16,256]{0,1:T(8,128)}, s32[16,256]{0,1:T(8,128)}, s32[16,256]{0,1:T(8,128)}, s32[16,256]{0,1:T(8,128)}, ...) fusion(s32[16,256]{0,1:T(8,128)S(1)} %bitcast.260, s32[16,32]{1,0:T(8,128)S(1)} %fusion.78, ...), kind=kLoop, calls=%fused_computation.79 | loop fusion | flops 3506176 | bytes 788480 | tf_op jit(solution)/shard_map/reduce_sum | solution.py:64
  94.2 1.0 copy.121
  95.2 1.0 copy.115
  96.2 0.6 fusion.94
  96.8 1.0 copy.116
  97.8 1.0 copy.117
  98.8 1.0 copy.118
  99.7 1.0 copy.119
  100.9 0.2 broadcast_select_fusion
  101.1 0.8 stack.59.dest_ref
  101.9 34.4 %convert_bitcast_fusion = bf16[3,8,512,16,64]{2,4,3,0,1:T(8,128)(2,1)} fusion(bf16[8,512,1024]{2,1,0:T(8,128)(2,1)} %param.10, f32[8,512]{1,0:T(8,128)S(1)} %fusion.72, bf16[1024,3,16,64]{0,3,2,1:T(8,128)(2,1)} %all-gather.11.cloned.1.call-done), kind=kOutput, calls=%fused_computation.30 | convolution fusion | flops 25794969600 | bytes 39862272 | tf_op jit(solution)/shard_map/jvp(bsd,dthe->tbshe)/dot_general | solution.py:28
  136.3 57.1 %fusion.95 = (f32[8,16,512]{2,1,0:T(8,128)S(1)}, f32[8,16,512,512]{2,3,1,0:T(8,128)}) fusion(pred[512,512]{0,1:T(8,128)(4,1)S(1)} %copy-done.20, bf16[3,8,512,16,64]{2,4,3,0,1:T(8,128)(2,1)} %convert_bitcast_fusion), kind=kOutput, calls=%fused_computation.182 | convolution fusion | flops 4429185536 | bytes 151519232 | tf_op jit(solution)/shard_map/jvp()/sub | solution.py:31
  193.4 63.8 %divide_convert_fusion = bf16[8,16,512,512]{2,3,1,0:T(8,128)(2,1)} fusion(f32[8,16,512,512]{2,3,1,0:T(8,128)} %get-tuple-element.104, f32[8,16,512]{2,1,0:T(8,128)S(1)} %get-tuple-element.103), kind=kLoop, calls=%fused_computation.9 | loop fusion | flops 67108864 | bytes 201588736 | tf_op jit(solution)/shard_map/jvp()/convert_element_type | solution.py:31
  257.2 29.5 %fusion.111 = bf16[8,512,16,64]{1,3,2,0:T(8,128)(2,1)} fusion(bf16[8,16,512,512]{2,3,1,0:T(8,128)(2,1)} %divide_convert_fusion, bf16[3,8,512,16,64]{2,4,3,0,1:T(8,128)(2,1)} %convert_bitcast_fusion), kind=kOutput, calls=%fused_computation.50.clone.1 | convolution fusion | flops 4299161600 | bytes 83886080 | tf_op jit(solution)/shard_map/jvp(bhqk,bkhe->bqhe)/dot_general | solution.py:32
  286.7 16.1 fusion.21
  302.9 84.9 %dispatch.1 = (bf16[32,1536,1024]{2,1,0:T(8,128)(2,1)}, bf16[32,1536,1024]{2,1,0:T(8,128)(2,1)}) custom-call(s32[16,32]{1,0:T(8,128)} %get-tuple-element.102.start_ref, s32[16,32]{1,0:T(8,128)} %copy-done.24, s32[16,32]{1,0:T(8,128)} %get-tuple-element.101.off_ref, bf16[4096,1024]{1,0:T(8,128)(2,1)} %bitcast.289, bf16[4096,1024]{1,0:T(8,128)(2,1)} %bitcast.286, ...), custom_call_target="tpu_custom_call" | custom-call | flops 80000000000 | bytes 180000000 | tf_op jit(solution)/shard_map/dispatch/pallas_call | solution.py:142
  387.9 130.4 %experts.4 = (bf16[32,1536,1024]{2,1,0:T(8,128)(2,1)}, bf16[32,1536,1024]{2,1,0:T(8,128)(2,1)}, f32[2,4,3,2,512,512]{5,4,3,2,1,0:T(8,128)}) custom-call(s32[32]{0:T(128)} %get-tuple-element.45.count_ref, bf16[32,1536,1024]{2,1,0:T(8,128)(2,1)} %get-tuple-element.21.r_ref, ...), custom_call_target="tpu_custom_call", output_to_operand_aliasing={{0}: (1, {}), {1}: (2, {})} | custom-call | flops 109999996928 | bytes 200000000 | tf_op jit(solution)/shard_map/experts/pallas_call | solution.py:215
  518.4 109.8 %experts.5 = (bf16[32,1536,1024]{2,1,0:T(8,128)(2,1)}, bf16[32,1536,1024]{2,1,0:T(8,128)(2,1)}, f32[2,4,3,2,512,512]{5,4,3,2,1,0:T(8,128)}) custom-call(s32[32]{0:T(128)} %get-tuple-element.45.count_ref, bf16[32,1536,1024]{2,1,0:T(8,128)(2,1)} %get-tuple-element.23.r_ref, ...), custom_call_target="tpu_custom_call", output_to_operand_aliasing={{0}: (1, {}), {1}: (2, {})} | custom-call | flops 109999996928 | bytes 200000000 | tf_op jit(solution)/shard_map/experts/pallas_call | solution.py:215
  628.3 108.5 %experts.6 = (bf16[32,1536,1024]{2,1,0:T(8,128)(2,1)}, bf16[32,1536,1024]{2,1,0:T(8,128)(2,1)}, f32[2,4,3,2,512,512]{5,4,3,2,1,0:T(8,128)}) custom-call(s32[32]{0:T(128)} %get-tuple-element.45.count_ref, bf16[32,1536,1024]{2,1,0:T(8,128)(2,1)} %get-tuple-element.25.r_ref, ...), custom_call_target="tpu_custom_call", output_to_operand_aliasing={{0}: (1, {}), {1}: (2, {})} | custom-call | flops 109999996928 | bytes 200000000 | tf_op jit(solution)/shard_map/experts/pallas_call | solution.py:215
  736.8 0.9 copy-done.18
  737.7 0.7 multiply_divide_fusion
  738.4 110.3 %experts.7 = (bf16[32,1536,1024]{2,1,0:T(8,128)(2,1)}, bf16[32,1536,1024]{2,1,0:T(8,128)(2,1)}, f32[2,4,3,2,512,512]{5,4,3,2,1,0:T(8,128)}) custom-call(s32[32]{0:T(128)} %get-tuple-element.45.count_ref, bf16[32,1536,1024]{2,1,0:T(8,128)(2,1)} %get-tuple-element.27.r_ref, ...), custom_call_target="tpu_custom_call", output_to_operand_aliasing={{0}: (1, {}), {1}: (2, {})} | custom-call | flops 109999996928 | bytes 200000000 | tf_op jit(solution)/shard_map/experts/pallas_call | solution.py:215
  848.7 101.3 %combine.1 = (bf16[4096,1024]{1,0:T(8,128)(2,1)}, bf16[4096,1024]{1,0:T(8,128)(2,1)}) custom-call(s32[16,32]{1,0:T(8,128)} %get-tuple-element.102.start_ref, s32[16,32]{1,0:T(8,128)} %copy-done.24, s32[16,32]{1,0:T(8,128)} %get-tuple-element.101.off_ref, bf16[32,1536,1024]{2,1,0:T(8,128)(2,1)} %get-tuple-element.29.y_hbm, ...), custom_call_target="tpu_custom_call" | custom-call | flops 89999998976 | bytes 180000000 | tf_op jit(solution)/shard_map/combine/pallas_call | solution.py:305
  950.1 12.9 convolution_convert_fusion.1
  963.0 71.3 %fusion.6 = (f32[8,16,512]{2,1,0:T(8,128)S(1)}, bf16[8,16,512,512]{2,3,1,0:T(8,128)(2,1)}) fusion(f32[8,16,512,512]{2,3,1,0:T(8,128)} %get-tuple-element.104, f32[8,16,512]{2,1,0:T(8,128)S(1)} %copy-done.9, bf16[3,8,512,16,64]{2,4,3,0,1:T(8,128)(2,1)} %convert_bitcast_fusion, bf16[8,512,16,64]{1,3,2,0:T(8,128)(2,1)S(1)} %convolution_convert_fusion.1), kind=kOutput, calls=%fused_computation.8 | convolution fusion | flops 4462673920 | bytes 218628096 | tf_op jit(solution)/shard_map/transpose(jvp(bhqk,bkhe->bqhe))/dot_general | solution.py:32
  1034.4 33.6 %convert_bitcast_fusion.3 = bf16[1,8,512,16,64]{2,4,3,1,0:T(8,128)(2,1)} fusion(bf16[8,16,512,512]{2,3,1,0:T(8,128)(2,1)} %divide_convert_fusion, bf16[8,512,16,64]{1,3,2,0:T(8,128)(2,1)S(1)} %convolution_convert_fusion.1), kind=kOutput, calls=%fused_computation.53 | convolution fusion | flops 4299161600 | bytes 83886080 | tf_op jit(solution)/shard_map/transpose(jvp(bhqk,bkhe->bqhe))/dot_general | solution.py:32
  1067.9 67.6 %convert_bitcast_fusion.1 = bf16[1,8,512,16,64]{2,4,3,1,0:T(8,128)(2,1)} fusion(bf16[3,8,512,16,64]{2,4,3,0,1:T(8,128)(2,1)} %convert_bitcast_fusion, f32[8,16,512,512]{2,3,1,0:T(8,128)} %get-tuple-element.104, bf16[8,16,512,512]{2,3,1,0:T(8,128)(2,1)} %get-tuple-element.106, f32[8,16,512]{2,1,0:T(8,128)S(1)} %neg.6, f32[8,16,512]{2,1,0:T(8,128)S(1)} %copy-done.19, ...), kind=kOutput, calls=%fused_computation.51 | convolution fusion | flops 4500488192 | bytes 218890240 | tf_op jit(solution)/shard_map/transpose(jvp(bqhe,bkhe->bhqk))/dot_general | solution.py:29
  1135.6 68.7 %convert_bitcast_fusion.2 = bf16[1,8,512,16,64]{2,4,3,1,0:T(8,128)(2,1)} fusion(bf16[3,8,512,16,64]{2,4,3,0,1:T(8,128)(2,1)} %convert_bitcast_fusion, f32[8,16,512,512]{2,3,1,0:T(8,128)} %get-tuple-element.104, bf16[8,16,512,512]{2,3,1,0:T(8,128)(2,1)} %get-tuple-element.106, f32[8,16,512]{2,1,0:T(8,128)S(1)} %neg.6, f32[8,16,512]{2,1,0:T(8,128)S(1)} %copy-done.19, ...), kind=kOutput, calls=%fused_computation.52 | convolution fusion | flops 4500488192 | bytes 218890240 | tf_op jit(solution)/shard_map/transpose(jvp(bqhe,bkhe->bhqk))/dot_general | solution.py:29
  1204.3 35.3 %fusion.22 = (f32[8,512]{1,0:T(8,128)S(1)}, bf16[8,512,1024]{2,1,0:T(8,128)(2,1)}) fusion(bf16[8,512,1024]{2,1,0:T(8,128)(2,1)S(1)} %copy-done, bf16[1024,3,16,64]{0,3,2,1:T(8,128)(2,1)} %all-gather.11.cloned.1.call-done, bf16[1,8,512,16,64]{2,4,3,1,0:T(8,128)(2,1)} %convert_bitcast_fusion.1, bf16[1,8,512,16,64]{2,4,3,1,0:T(8,128)(2,1)} %convert_bitcast_fusion.2, ...), kind=kOutput, calls=%fused_computation.36 | convolution fusion | flops 25815937024 | bytes 48250880 | tf_op jit(solution)/shard_map/transpose(jvp(bsd,dthe->tbshe))/dot_general | solution.py:28
  1239.6 11.3 fusion.29
  1250.9 5.9 slice_bitcast_fusion.21
  1256.7 5.7 slice_bitcast_fusion.20
  1262.5 178.3 %reduce-scatter.9.cloned.1.call-done = f32[1,3,2,512,512]{4,3,2,1,0:T(8,128)} async-done(((f32[8,3,2,512,512]{4,3,2,1,0:T(8,128)}), f32[1,3,2,512,512]{4,3,2,1,0:T(8,128)}) %reduce-scatter.9.cloned.1.call-update) | async-done | bytes 6291472 | tf_op jit(solution)/shard_map/reduce_scatter | solution.py:369
  1440.8 5.7 slice_bitcast_fusion.19
  1446.5 272.2 %reduce-scatter.11.cloned.1.call-done = f32[1,3,2,512,512]{4,3,2,1,0:T(8,128)} async-done(((f32[8,3,2,512,512]{4,3,2,1,0:T(8,128)}), f32[1,3,2,512,512]{4,3,2,1,0:T(8,128)}) %reduce-scatter.11.cloned.1.call-update) | async-done | bytes 6291472 | tf_op jit(solution)/shard_map/reduce_scatter | solution.py:369
  1718.7 4.4 slice_bitcast_fusion.18
  1723.1 0.3 copy-done.8
  1723.5 4.6 pad_maximum_fusion.2
  1728.1 1.1 copy-done.7
  1729.2 4.1 pad_maximum_fusion.1
  1733.3 3.9 pad_maximum_fusion
  (108 shorter events, 3.0 us)
Async XLA Ops:
  7.2 94.8 %all-gather.11.cloned.1.call-start = ((), (), s32[]{:S(2)}) async-start(), calls=%async_computation.4 | async-start | bytes 9437184 | tf_op jit(solution)/shard_map/all_gather | solution.py:347
  7.9 278.8 %all-gather.13.cloned.1.call-start = ((), (), s32[]{:S(2)}) async-start(), calls=%async_computation.5 | async-start | bytes 3145728 | tf_op jit(solution)/shard_map/all_gather | solution.py:348
  8.6 379.2 %all-gather.15.cloned.1.call-start = ((), (), s32[]{:S(2)}) async-start(), calls=%async_computation.10 | async-start | bytes 28311552 | tf_op jit(solution)/shard_map/all_gather | solution.py:353
  8.7 4.2 copy-start.10
  8.7 5.9 copy-start.11
  18.5 499.9 %all-gather.17.cloned.1.call-start = ((), (), s32[]{:S(2)}) async-start(), calls=%async_computation.11 | async-start | bytes 28311552 | tf_op jit(solution)/shard_map/all_gather | solution.py:353
  22.4 605.9 %all-gather.19.cloned.1.call-start = ((), (), s32[]{:S(2)}) async-start(), calls=%async_computation.12 | async-start | bytes 28311552 | tf_op jit(solution)/shard_map/all_gather | solution.py:353
  22.5 8.3 copy-start.25
  26.1 5.7 copy-start.26
  26.1 712.4 %all-gather.21.cloned.1.call-start = ((), (), s32[]{:S(2)}) async-start(), calls=%async_computation.13 | async-start | bytes 28311552 | tf_op jit(solution)/shard_map/all_gather | solution.py:353
  29.4 1221.4 %reduce-scatter.5.cloned.1.call-start = ((), (), s32[]{:S(2)}) async-start(), calls=%async_computation.6 | async-start | bytes 56623104 | tf_op jit(solution)/shard_map/reduce_scatter | solution.py:369
  31.6 1.4 copy-start.13
  31.7 1.3 copy-start.15
  42.3 9.2 copy-start.29
  44.1 9.4 copy-start.14
  44.1 9.4 copy-start.16
  44.2 1.3 copy-start.12
  46.2 90.1 %copy-start.24 = (s32[16,32]{1,0:T(8,128)}, s32[16,32]{1,0:T(8,128)S(1)}, u32[]{:S(2)}) copy-start(s32[16,32]{1,0:T(8,128)S(1)} %get-tuple-element.46.rows_ref) | copy-start | bytes 6148
  51.5 0.6 copy-start.22
  51.5 84.8 %copy-start.27 = (f32[8,512]{1,0:T(8,128)}, f32[8,512]{1,0:T(8,128)S(1)}, u32[]{:S(2)}) copy-start(f32[8,512]{1,0:T(8,128)S(1)} %fusion.72) | copy-start | bytes 49156
  101.9 34.4 %copy-start.20 = (pred[512,512]{0,1:T(8,128)(4,1)S(1)}, pred[512,512]{0,1:T(8,128)(4,1)}, u32[]{:S(2)}) copy-start(pred[512,512]{0,1:T(8,128)(4,1)} %iota_compare_fusion.8) | copy-start | bytes 786436
  193.4 63.8 %copy-start.17 = (f32[8,16,512]{2,1,0:T(8,128)}, f32[8,16,512]{2,1,0:T(8,128)S(1)}, u32[]{:S(2)}) copy-start(f32[8,16,512]{2,1,0:T(8,128)S(1)} %get-tuple-element.103) | copy-start | bytes 786436
  518.3 738.5 %reduce-scatter.7.cloned.1.call-start = ((), (), s32[]{:S(2)}) async-start(), calls=%async_computation.7 | async-start | bytes 56623104 | tf_op jit(solution)/shard_map/reduce_scatter | solution.py:369
  628.2 812.5 %reduce-scatter.9.cloned.1.call-start = ((), (), s32[]{:S(2)}) async-start(), calls=%async_computation.8 | async-start | bytes 56623104 | tf_op jit(solution)/shard_map/reduce_scatter | solution.py:369
  736.7 1.0 copy-start.18
  736.8 981.9 %reduce-scatter.11.cloned.1.call-start = ((), (), s32[]{:S(2)}) async-start(), calls=%async_computation.9 | async-start | bytes 56623104 | tf_op jit(solution)/shard_map/reduce_scatter | solution.py:369
  950.1 12.9 copy-start.9
  1034.3 33.6 %copy-start.19 = (f32[8,16,512]{2,1,0:T(8,128)S(1)}, f32[8,16,512]{2,1,0:T(8,128)}, u32[]{:S(2)}) copy-start(f32[8,16,512]{2,1,0:T(8,128)} %copy-done.17) | copy-start | bytes 786436
  1034.4 33.6 %copy-start.21 = (pred[512,512]{0,1:T(8,128)(4,1)S(1)}, pred[512,512]{0,1:T(8,128)(4,1)}, u32[]{:S(2)}) copy-start(pred[512,512]{0,1:T(8,128)(4,1)} %iota_compare_fusion.8) | copy-start | bytes 786436
  1135.6 68.7 %copy-start = (bf16[8,512,1024]{2,1,0:T(8,128)(2,1)S(1)}, bf16[8,512,1024]{2,1,0:T(8,128)(2,1)}, u32[]{:S(2)}) copy-start(bf16[8,512,1024]{2,1,0:T(8,128)(2,1)} %param.10) | copy-start | bytes 25165828
  1204.3 35.3 %copy-start.23 = (f32[8,512]{1,0:T(8,128)S(1)}, f32[8,512]{1,0:T(8,128)}, u32[]{:S(2)}) copy-start(f32[8,512]{1,0:T(8,128)} %copy-done.22) | copy-start | bytes 49156
  1204.3 35.3 %copy-start.28 = (f32[8,512]{1,0:T(8,128)S(1)}, f32[8,512]{1,0:T(8,128)}, u32[]{:S(2)}) copy-start(f32[8,512]{1,0:T(8,128)} %copy-done.27) | copy-start | bytes 49156
  1718.7 4.4 copy-start.3
  1718.7 4.4 copy-start.6
  1718.7 4.7 copy-start.8
  1723.4 4.6 copy-start.1
  1723.4 4.6 copy-start.4
  1723.4 5.8 copy-start.7
  1729.2 4.1 copy-start.2
  1729.2 4.1 copy-start.5
Sparse Core Ops, SparseCore 0:
  9.5 77.9 all-gather.10
  89.0 30.1 all-gather.12
  121.6 120.2 all-gather.14
  244.2 119.6 all-gather.16
  366.1 119.6 all-gather.18
  487.4 119.6 all-gather.20
  610.6 273.8 reduce-scatter.4
  888.1 274.5 reduce-scatter.6
  1166.2 274.5 reduce-scatter.8
  1444.2 274.5 reduce-scatter.10
